TPU v7x, 32 devices: a whole 2x2x4 slice. The times are simulated.
32 devices in a mesh: member: 4 (over y, x), space: 8 (over z, core).
Axes of the slice: x: 2, y: 2, z: 4, core: 2. Of those that a mesh axis runs over, the one named last changes fastest.
Arguments:
- ensemble_prediction: bfloat16 [4, 300, 128, 128], P('member', None, 'space'), may hold values from -6 to 6
- observed_analysis: bfloat16 [300, 128, 128], P(None, 'space'), may hold values from -6 to 6
- validity_flags: int32 [2, 128, 128], P(None, 'space'), may hold values from 0 to 1, as said below
Outputs:
- point_score: float32 [300, 128, 128], P(None, 'space')
- channel_loss: float32 [300], replicated
Inputs may be any that keep to these rules, and one draw needn't show every extreme that they name: `validity_flags`: 0 or 1 for each point and group; every point of latitude row 11 is valid in both groups.
All inputs are finite; a program needn't handle non-finite values.
Results may differ from a plain program's by a relative error of at most 0.0003.
Values may be sent and summed in bfloat16 or wider, within the bound.
A program may use at most 64 MiB of HBM per device.

v0:
```python
import jax
import jax.numpy as jnp
from jax import lax
from jax.sharding import PartitionSpec as P

VARIABLE_NUMBER = 300
ATMOS = 180
TILE_SITES = 128
LON = 720
ROWS = 360


def per_channel(values):
    is_ocean = jnp.arange(VARIABLE_NUMBER, dtype=jnp.int32) >= ATMOS
    return jnp.where(is_ocean, values[1], values[0])


def shards(ensemble_prediction, observed_analysis, validity_flags):
    blocks_here = observed_analysis.shape[1]
    realization_entries = lax.axis_size("member")
    lat_rows = min(ROWS, blocks_here * lax.axis_size("space") * TILE_SITES // LON)
    first_point = lax.axis_index("space") * (blocks_here * TILE_SITES)
    position = first_point + jnp.arange(blocks_here * TILE_SITES, dtype=jnp.int32).reshape(
        blocks_here, TILE_SITES
    )
    inside = (position < lat_rows * LON).astype(jnp.float32)
    lat_row = (position // LON).astype(jnp.float32)
    cosine = jnp.cos(jnp.pi * ((lat_row + 0.5) / lat_rows - 0.5))
    valid = inside[None] * (validity_flags > 0).astype(jnp.float32)
    weight = cosine[None] * valid
    local_area = jnp.sum(weight, axis=(1, 2))
    local_count = jnp.sum(valid, axis=(1, 2))
    is_ocean = jnp.arange(VARIABLE_NUMBER, dtype=jnp.int32) >= ATMOS
    weight_chan = jnp.where(is_ocean[:, None, None], weight[1][None], weight[0][None])
    coeff = (1.0 - 0.05 / realization_entries) / (
        2.0 * realization_entries * (realization_entries - 1)
    )
    gathered = lax.all_to_all(
        ensemble_prediction, "member", split_axis=2, concat_axis=0, tiled=True
    )
    share = blocks_here // realization_entries
    first_block = lax.axis_index("member") * share
    target_part = lax.dynamic_slice_in_dim(observed_analysis, first_block, share, 1).astype(
        jnp.float32
    )
    accuracy_component = jnp.zeros(target_part.shape, jnp.float32)
    dispersion_component = jnp.zeros(target_part.shape, jnp.float32)
    for leading_realization in range(realization_entries):
        lead = gathered[leading_realization].astype(jnp.float32)
        accuracy_component = accuracy_component + jnp.abs(lead - target_part)
        for trailing_realization in range(leading_realization + 1, realization_entries):
            dispersion_component = dispersion_component + jnp.abs(
                lead - gathered[trailing_realization].astype(jnp.float32)
            )
    partial_crps = accuracy_component / realization_entries - coeff * (2.0 * dispersion_component)
    crps = lax.all_gather(partial_crps, "member", axis=1, tiled=True)
    area_sum, count = lax.psum((local_area, local_count), "space")
    scale_chan = per_channel(count / area_sum)
    point_score = crps * weight_chan * scale_chan[:, None, None]
    score_sums = lax.psum(jnp.sum(point_score, axis=(1, 2)), "space")
    channel_loss = score_sums / per_channel(count)
    return (point_score, channel_loss)


def solution(mesh):
    in_specs = (P("member", None, "space", None), P(None, "space", None), P(None, "space", None))
    out_specs = (P(None, "space", None), P())
    return jax.shard_map(shards, mesh=mesh, in_specs=in_specs, out_specs=out_specs, check_vma=False)
```

profile of v0, /device:TPU:0, one launch (start us, length us, event | category | flops | bytes accessed | tf_op | source)
XLA Modules:
  0.0 100.8 jit_solution(2808371847547564155)
XLA Ops:
  7.2 0.0 copy-start
  7.2 2.7 %copy.11 = bf16[1,300,16,128]{3,1,0,2:T(8,128)(2,1)} copy(bf16[1,300,16,128]{3,2,1,0:T(8,128)(2,1)} %param.3) | data formatting | bytes 2457600 | tf_op args[0]
  9.9 0.0 copy-start.1
  9.9 5.3 %all-to-all-start = ((bf16[1,300,16,128]{3,1,0,2:T(8,128)(2,1)}), bf16[1,300,16,128]{3,1,0,2:T(8,128)(2,1)S(1)}, u32[]{:S(2)}, u32[]{:S(2)}) async-start(bf16[1,300,16,128]{3,1,0,2:T(8,128)(2,1)} %copy.11), calls=%async_computation | async-start | bytes 2490368 | tf_op jit(solution)/shard_map/all_to_all | solution.py:38
  15.2 0.0 all-gather.2.cloned.1.call-start
  15.2 0.0 copy-done
  15.2 0.2 constant_dynamic-slice_fusion
  15.4 15.6 %all-to-all-done = bf16[1,300,16,128]{3,1,0,2:T(8,128)(2,1)S(1)} async-done(((bf16[1,300,16,128]{3,1,0,2:T(8,128)(2,1)}), bf16[1,300,16,128]{3,1,0,2:T(8,128)(2,1)S(1)}, u32[]{:S(2)}, u32[]{:S(2)}) %all-to-all-start) | async-done | bytes 1228832 | tf_op jit(solution)/shard_map/all_to_all | solution.py:38
  31.0 1.6 %fusion.5 = f32[300,4,128]{2,0,1:T(8,128)} fusion(bf16[4,1,300,4,128]{4,2,3,0,1:T(8,128)(2,1)S(1)} %bitcast.33, bf16[4,1,300,4,128]{4,2,3,1,0:T(8,128)(2,1)S(1)} %bitcast.34, bf16[300,4,128]{2,1,0:T(4,128)(2,1)S(1)} %constant_dynamic-slice_fusion), kind=kLoop, calls=%fused_computation.16 | loop fusion | flops 5529600 | bytes 2150400 | tf_op jit(solution)/shard_map/sub | solution.py:55
  32.5 0.0 all-gather.2.cloned.1.call-update
  32.6 0.1 fusion.26
  32.7 0.0 copy-done.1
  32.7 0.1 fusion.31
  32.8 0.1 select_reduce_fusion
  32.9 15.9 %all-reduce = (f32[2]{0:T(128)S(1)}, f32[2]{0:T(128)S(1)}) all-reduce(f32[2]{0:T(128)S(1)} %select_reduce_fusion, f32[2]{0:T(128)S(1)} %get-tuple-element.10), channel_id=1, replica_groups=mesh['member'=4,'space'=8] {'space'}, use_global_device_ids=true, to_apply=%region_1.2 | all-reduce | flops 4 | bytes 32 | tf_op jit(solution)/shard_map/psum | solution.py:57
  48.8 0.6 fusion.33
  49.4 1.3 %broadcast_select_fusion = f32[300]{0:T(512)S(1)} fusion(f32[]{:T(128)} %bitcast.16, f32[]{:T(128)} %bitcast.15), kind=kLoop, calls=%fused_computation.56 | loop fusion | flops 600 | bytes 1208 | tf_op jit(solution)/shard_map/jit(_where)/select_n | solution.py:15
  50.7 0.6 fusion.32
  51.3 20.2 %all-gather.2.cloned.1.call-done = f32[300,16,128]{2,0,1:T(8,128)} async-done(((f32[300,4,128]{2,0,1:T(8,128)}), f32[300,16,128]{2,0,1:T(8,128)}) %all-gather.2.cloned.1.call-update) | async-done | bytes 2457616 | tf_op jit(solution)/shard_map/all_gather | solution.py:56
  71.5 2.2 %fusion.30 = (f32[300]{0:T(512)S(1)}, f32[300,16,128]{2,0,1:T(8,128)S(1)}) fusion(f32[300]{0:T(512)S(1)} %broadcast_select_fusion, f32[300,16,128]{2,0,1:T(8,128)} %all-gather.2.cloned.1.call-done, f32[16,128]{1,0:T(8,128)S(1)} %get-tuple-element.14, f32[16,128]{1,0:T(8,128)S(1)} %get-tuple-element.13, pred[300]{0:T(512)(128)(4,1)S(1)} %iota_compare_fusion), kind=kLoop, calls=%fused_computation.58 | loop fusion | flops 2457300 | bytes 4934284 | tf_op jit(solution)/shard_map/reduce_sum | solution.py:60
  73.7 2.2 %copy.16 = f32[300,16,128]{2,1,0:T(8,128)} copy(f32[300,16,128]{2,0,1:T(8,128)S(1)} %get-tuple-element.9) | data formatting | bytes 4915200
  75.9 16.2 %psum.23 = f32[300]{0:T(512)S(1)} all-reduce(f32[300]{0:T(512)S(1)} %get-tuple-element.8), channel_id=1, replica_groups=mesh['member'=4,'space'=8] {'space'}, use_global_device_ids=true, to_apply=%region_5.6 | all-reduce | flops 300 | bytes 2400 | tf_op jit(solution)/shard_map/psum | solution.py:60
  92.1 1.9 %select_divide_fusion = f32[300]{0:T(512)} fusion(f32[300]{0:T(512)S(1)} %psum.23, f32[]{:T(128)} %bitcast.18, f32[]{:T(128)} %bitcast.17), kind=kLoop, calls=%fused_computation.54 | loop fusion | flops 900 | bytes 2408 | tf_op jit(solution)/shard_map/div | solution.py:61
  (4 shorter events, 0.0 us)
Async XLA Ops:
  7.2 8.1 %copy-start = (bf16[300,16,128]{2,1,0:T(8,128)(2,1)S(1)}, bf16[300,16,128]{2,1,0:T(8,128)(2,1)}, u32[]{:S(2)}) copy-start(bf16[300,16,128]{2,1,0:T(8,128)(2,1)} %param.4) | copy-start | bytes 3686404
  9.9 22.7 %copy-start.1 = (s32[2,16,128]{2,1,0:T(8,128)S(1)}, s32[2,16,128]{2,1,0:T(8,128)}, u32[]{:S(2)}) copy-start(s32[2,16,128]{2,1,0:T(8,128)} %param.5) | copy-start | bytes 49156
  9.9 21.1 %all-to-all-start = ((bf16[1,300,16,128]{3,1,0,2:T(8,128)(2,1)}), bf16[1,300,16,128]{3,1,0,2:T(8,128)(2,1)S(1)}, u32[]{:S(2)}, u32[]{:S(2)}) async-start(bf16[1,300,16,128]{3,1,0,2:T(8,128)(2,1)} %copy.11), calls=%async_computation | async-start | bytes 2490368 | tf_op jit(solution)/shard_map/all_to_all | solution.py:38
  15.2 56.2 %all-gather.2.cloned.1.call-start = ((), (), s32[]{:S(2)}) async-start(), calls=%async_computation.1 | async-start | bytes 3112960 | tf_op jit(solution)/shard_map/all_gather | solution.py:56
Sparse Core Ops, SparseCore 0:
  32.7 38.7 all-gather.1
where the time goes:
time: 101 us
  waiting for transfers between devices  35.8 us (35%)
  blocking collectives  32.1 us (32%)
  between operations  14.1 us (14%)
  other arithmetic  7.25 us (7%)
  local copies, waits for them, and re-layouts  6.33 us (6%)
  starting transfers between devices  5.33 us (5%)
    all_gather x1, waiting for transfers between devices, shards(): crps = lax.all_gather(partial_crps, 'member', axis=1, tiled=True)  20.2 us
    psum x1, blocking collectives, shards(): score_sums = lax.psum(jnp.sum(point_score, axis=(1, 2)), 'space')  16.2 us
    psum x1, blocking collectives, shards(): area_sum, count = lax.psum((local_area, local_count), 'space')  15.9 us
    all_to_all x1, waiting for transfers between devices, shards(): lax.all_to_all(ensemble_prediction, 'member', split_axis=2, concat_axis=0...  15.6 us
    all_to_all x1, starting transfers between devices, shards(): lax.all_to_all(ensemble_prediction, 'member', split_axis=2, concat_axis=0...  5.32 us
    unnamed x6, local copies, waits for them, and re-layouts  4.95 us
    reduce_sum x1, other arithmetic, shards(): score_sums = lax.psum(jnp.sum(point_score, axis=(1, 2)), 'space')  2.23 us
  transfers between devices with their start and end apart: 2, of which 2 were waited for; matrix products, arithmetic and copies ran while one was open for 3% of the time, Pallas kernels for 0%

commit v1 on v0

--- a/solution.py
+++ b/solution.py
@@ -53,7 +53,12 @@
                 lead - gathered[trailing_realization].astype(jnp.float32)
             )
     partial_crps = accuracy_component / realization_entries - coeff * (2.0 * dispersion_component)
-    crps = lax.all_gather(partial_crps, "member", axis=1, tiled=True)
+    crps = jnp.concatenate(
+        jax.lax.all_to_all(
+            jnp.stack([partial_crps for _ in range(jax.lax.axis_size("member"))], 0), "member", 0, 0
+        ),
+        1,
+    )
     area_sum, count = lax.psum((local_area, local_count), "space")
     scale_chan = per_channel(count / area_sum)
     point_score = crps * weight_chan * scale_chan[:, None, None]

time: 101 us -> 88.7 us (0.88)
  between operations: 14.1 us -> 0.71 us
  waiting for transfers between devices: 35.8 us -> 25.1 us
  starting transfers between devices: 5.33 us -> 9.83 us
  local copies, waits for them, and re-layouts: 6.33 us -> 10.2 us
  other arithmetic: 7.25 us -> 10.5 us
    all_gather x1 -> x0, waiting for transfers between devices: 20.2 us -> none  [shards(): crps = lax.all_gather(partial_crps, 'member', axis=1, tiled=True)]
    all_to_all x0 -> x1, waiting for transfers between devices: none -> 9.56 us  [shards(): jax.lax.all_to_all(jnp.stack([partial_crps for _ in range(jax.lax.axis_si...]
    all_to_all x0 -> x1, starting transfers between devices: none -> 4.64 us  [shards(): jax.lax.all_to_all(jnp.stack([partial_crps for _ in range(jax.lax.axis_si...]
    reduce_sum x1, other arithmetic: 2.23 us -> 5.98 us  [shards(): score_sums = lax.psum(jnp.sum(point_score, axis=(1, 2)), 'space')]
    reshape x0 -> x1, local copies, waits for them, and re-layouts: none -> 1.86 us  [shards(): jnp.concatenate(jax.lax.all_to_all(jnp.stack([partial_crps for _ in range...]
    another operation x0 -> x1, local copies, waits for them, and re-layouts: none -> 1.75 us  [shards(): jnp.stack([partial_crps for _ in range(jax.lax.axis_size('member'))], 0)]
where the time goes in v1:
time: 88.7 us; the launch traced here: 88.2 us
  blocking collectives  31.8 us (36%)
  waiting for transfers between devices  25.1 us (28%)
  other arithmetic  10.5 us (12%)
  local copies, waits for them, and re-layouts  10.2 us (11%)
  starting transfers between devices  9.83 us (11%)
    psum x1, blocking collectives, shards(): score_sums = lax.psum(jnp.sum(point_score, axis=(1, 2)), 'space')  15.9 us
    psum x1, blocking collectives, shards(): area_sum, count = lax.psum((local_area, local_count), 'space')  15.9 us
    all_to_all x1, waiting for transfers between devices, shards(): lax.all_to_all(ensemble_prediction, 'member', split_axis=2, concat_axis=0...  15.6 us
    all_to_all x1, waiting for transfers between devices, shards(): jax.lax.all_to_all(jnp.stack([partial_crps for _ in range(jax.lax.axis_si...  9.56 us
    reduce_sum x1, other arithmetic, shards(): score_sums = lax.psum(jnp.sum(point_score, axis=(1, 2)), 'space')  5.98 us
    all_to_all x1, starting transfers between devices, shards(): lax.all_to_all(ensemble_prediction, 'member', split_axis=2, concat_axis=0...  5.19 us
    unnamed x6, local copies, waits for them, and re-layouts  4.94 us
    all_to_all x1, starting transfers between devices, shards(): jax.lax.all_to_all(jnp.stack([partial_crps for _ in range(jax.lax.axis_si...  4.64 us
  transfers between devices with their start and end apart: 2, of which 2 were waited for; matrix products, arithmetic and copies ran while one was open for 3% of the time, Pallas kernels for 0%

profile of v1, /device:TPU:0, one launch (start us, length us, event | category | flops | bytes accessed | tf_op | source)
XLA Modules:
  0.0 88.2 jit_solution(16575185337014243346)
XLA Ops:
  0.6 0.0 copy-start
  0.6 2.7 %copy.17 = bf16[1,300,16,128]{3,1,0,2:T(8,128)(2,1)} copy(bf16[1,300,16,128]{3,2,1,0:T(8,128)(2,1)} %param.3) | data formatting | bytes 2457600 | tf_op args[0]
  3.4 5.2 %all-to-all-start = ((bf16[1,300,16,128]{3,1,0,2:T(8,128)(2,1)}), bf16[1,300,16,128]{3,1,0,2:T(8,128)(2,1)S(1)}, u32[]{:S(2)}, u32[]{:S(2)}) async-start(bf16[1,300,16,128]{3,1,0,2:T(8,128)(2,1)} %copy.17), calls=%async_computation | async-start | bytes 2490368 | tf_op jit(solution)/shard_map/all_to_all | solution.py:38
  8.6 0.0 copy-done
  8.6 0.2 constant_dynamic-slice_fusion
  8.7 15.6 %all-to-all-done = bf16[1,300,16,128]{3,1,0,2:T(8,128)(2,1)S(1)} async-done(((bf16[1,300,16,128]{3,1,0,2:T(8,128)(2,1)}), bf16[1,300,16,128]{3,1,0,2:T(8,128)(2,1)S(1)}, u32[]{:S(2)}, u32[]{:S(2)}) %all-to-all-start) | async-done | bytes 1228832 | tf_op jit(solution)/shard_map/all_to_all | solution.py:38
  24.3 0.7 fusion.6
  25.0 0.2 copy.22
  25.3 1.8 %stack.2 = f32[4,300,4,128]{3,2,1,0:T(4,128)} broadcast(f32[300,4,128]{2,1,0:T(4,128)S(1)} %copy.22), dimensions={1,2,3} | broadcast | bytes 3072000 | tf_op jit(solution)/shard_map/stack | solution.py:58
  27.0 4.6 %all-to-all-start.1 = ((f32[4,300,4,128]{3,2,1,0:T(4,128)}), f32[4,300,4,128]{3,2,1,0:T(4,128)}, u32[]{:S(2)}, u32[]{:S(2)}) async-start(f32[4,300,4,128]{3,2,1,0:T(4,128)} %stack.2), calls=%async_computation.1 | async-start | bytes 4915200 | tf_op jit(solution)/shard_map/all_to_all | solution.py:57
  31.7 0.1 fusion.27
  31.8 0.1 fusion.31
  31.9 0.1 select_reduce_fusion
  32.0 15.9 %all-reduce = (f32[2]{0:T(128)S(1)}, f32[2]{0:T(128)S(1)}) all-reduce(f32[2]{0:T(128)S(1)} %select_reduce_fusion, f32[2]{0:T(128)S(1)} %get-tuple-element.6), channel_id=1, replica_groups=mesh['member'=4,'space'=8] {'space'}, use_global_device_ids=true, to_apply=%region_1.2 | all-reduce | flops 4 | bytes 32 | tf_op jit(solution)/shard_map/psum | solution.py:62
  47.9 0.6 fusion.34
  48.5 1.3 %broadcast_select_fusion = f32[300]{0:T(512)S(1)} fusion(f32[]{:T(128)} %bitcast.18, f32[]{:T(128)} %bitcast.17), kind=kLoop, calls=%fused_computation.56 | loop fusion | flops 600 | bytes 1208 | tf_op jit(solution)/shard_map/jit(_where)/select_n | solution.py:15
  49.8 0.6 fusion.33
  50.5 9.6 %all-to-all-done.1 = f32[4,300,4,128]{3,2,1,0:T(4,128)} async-done(((f32[4,300,4,128]{3,2,1,0:T(4,128)}), f32[4,300,4,128]{3,2,1,0:T(4,128)}, u32[]{:S(2)}, u32[]{:S(2)}) %all-to-all-start.1) | async-done | bytes 2457632 | tf_op jit(solution)/shard_map/all_to_all | solution.py:57
  60.0 6.0 %multiply_reduce_fusion = f32[300]{0:T(512)S(1)} fusion(f32[300]{0:T(512)S(1)} %broadcast_select_fusion, f32[4,4,128]{2,1,0:T(4,128)S(1)} %bitcast.44, f32[4,4,128]{2,1,0:T(4,128)S(1)} %bitcast.43, pred[300]{0:T(512)(128)(4,1)S(1)} %iota_compare_fusion, f32[4,300,4,128]{3,2,1,0:T(4,128)} %all-to-all-done.1), kind=kLoop, calls=%fused_computation.2 | loop fusion | flops 2457300 | bytes 2476684 | tf_op jit(solution)/shard_map/reduce_sum | solution.py:65
  66.0 15.9 %psum.23 = f32[300]{0:T(512)S(1)} all-reduce(f32[300]{0:T(512)S(1)} %multiply_reduce_fusion), channel_id=1, replica_groups=mesh['member'=4,'space'=8] {'space'}, use_global_device_ids=true, to_apply=%region_5.6 | all-reduce | flops 300 | bytes 2400 | tf_op jit(solution)/shard_map/psum | solution.py:65
  81.9 1.9 %copy.23 = f32[300,4,4,128]{3,0,2,1:T(8,128)S(1)} copy(f32[300,4,4,128]{3,2,0,1:T(4,128)} %bitcast.13) | data formatting | bytes 4915200 | tf_op jit(solution)/shard_map/reshape | solution.py:56
  83.8 0.4 fusion
  84.2 2.2 %copy.24 = f32[300,16,128]{2,1,0:T(8,128)} copy(f32[300,16,128]{2,0,1:T(8,128)S(1)} %fusion) | data formatting | bytes 4915200
  86.4 1.8 %select_divide_fusion = f32[300]{0:T(512)} fusion(f32[300]{0:T(512)S(1)} %psum.23, f32[]{:T(128)} %bitcast.22, f32[]{:T(128)} %bitcast.21), kind=kLoop, calls=%fused_computation.54 | loop fusion | flops 900 | bytes 2408 | tf_op jit(solution)/shard_map/div | solution.py:66
  (6 shorter events, 0.0 us)
Async XLA Ops:
  0.6 7.9 %copy-start = (bf16[300,16,128]{2,1,0:T(8,128)(2,1)S(1)}, bf16[300,16,128]{2,1,0:T(8,128)(2,1)}, u32[]{:S(2)}) copy-start(bf16[300,16,128]{2,1,0:T(8,128)(2,1)} %param.4) | copy-start | bytes 3686404
  3.4 20.9 %all-to-all-start = ((bf16[1,300,16,128]{3,1,0,2:T(8,128)(2,1)}), bf16[1,300,16,128]{3,1,0,2:T(8,128)(2,1)S(1)}, u32[]{:S(2)}, u32[]{:S(2)}) async-start(bf16[1,300,16,128]{3,1,0,2:T(8,128)(2,1)} %copy.17), calls=%async_computation | async-start | bytes 2490368 | tf_op jit(solution)/shard_map/all_to_all | solution.py:38
  27.0 4.7 %copy-start.1 = (s32[2,16,128]{2,1,0:T(8,128)S(1)}, s32[2,16,128]{2,1,0:T(8,128)}, u32[]{:S(2)}) copy-start(s32[2,16,128]{2,1,0:T(8,128)} %param.5) | copy-start | bytes 49156
  27.0 33.0 %all-to-all-start.1 = ((f32[4,300,4,128]{3,2,1,0:T(4,128)}), f32[4,300,4,128]{3,2,1,0:T(4,128)}, u32[]{:S(2)}, u32[]{:S(2)}) async-start(f32[4,300,4,128]{3,2,1,0:T(4,128)} %stack.2), calls=%async_computation.1 | async-start | bytes 4915200 | tf_op jit(solution)/shard_map/all_to_all | solution.py:57
